TPU v7x, 32 devices: a whole 2x2x4 slice. The times are simulated.
32 devices in a mesh: patch: 16 (over z, y, x), batch: 2 (over core).
Axes of the slice: x: 2, y: 2, z: 4, core: 2. Of those that a mesh axis runs over, the one named last changes fastest.
Arguments:
- tokens: bfloat16 [4096, 1152], P(('batch', 'patch')), parts along dimension 0, may hold values from -6 to 6
- slots: int32 [4096], P(('batch', 'patch')), parts along dimension 0, may hold values from 0 to 127, as said below
- counts: int32 [32], P(('batch', 'patch')), parts along dimension 0, may hold values from 32 to 128, as said below
- shift: float32 [1152], replicated, may hold values from -3 to 3
- scale: float32 [1152], replicated, may hold values from -3 to 3
- gate: float32 [1152], replicated, may hold values from -4 to 4
- w_qkv: bfloat16 [1152, 3456], replicated, may hold values from -1 to 1
- w_out: bfloat16 [1152, 1152], replicated, may hold values from -0.1875 to 0.1875
Outputs:
- result: bfloat16 [4096, 1152], P(('batch', 'patch')), parts along dimension 0
There are 2 independent parts, one for each index of `batch`. A program takes and returns all parts, laid end to end along the dimension named above; an argument that names none is the same for every part. Nothing has to cross between parts.
Inputs may be any that keep to these rules, and one draw needn't show every extreme that they name: `counts`: at least a quarter of each block's slots are live. The live slots of all blocks of an image number exactly 80 times the number of patch devices, and all blocks of some device are full. `slots`: every token's slot is below its block's count, and every slot below the count holds at least one token.
All inputs are finite; a program needn't handle non-finite values.
Results may differ from a plain program's by a relative error of at most 0.011.
Values may be sent and summed in bfloat16 or wider, within the bound.
A program may use at most 192 MiB of HBM per device.

v0:
```python
import jax
import jax.numpy as jnp
from jax import lax
from jax.sharding import PartitionSpec as P

HEADS = 16
BLK = 128


def layer_norm(merged, shift, scale):
    values = merged.astype(jnp.float32)
    center = jnp.mean(values, axis=-1, keepdims=True)
    spread = jnp.mean((values - center) ** 2, axis=-1, keepdims=True)
    return ((values - center) * lax.rsqrt(spread + 1e-06) * (1.0 + scale) + shift).astype(
        jnp.bfloat16
    )


def size_bias(sizes):
    return jnp.log(jnp.maximum(sizes.astype(jnp.float32), 1.0))


def empty_carry(heads, query_rows, head_size):
    return (
        jnp.full((heads, query_rows), -1e30, jnp.float32),
        jnp.zeros((heads, query_rows), jnp.float32),
        jnp.zeros((heads, query_rows, head_size), jnp.float32),
    )


def finish(accum, total):
    heads, query_rows, head_size = accum.shape
    return (
        (accum / total[:, :, None])
        .transpose(1, 0, 2)
        .reshape(query_rows, heads * head_size)
        .astype(jnp.bfloat16)
    )


def attend_piece(query, carry, keys, values, bias, inverse):
    top, total, accum = carry
    key_rows = keys.shape[0]
    heads = query.shape[1]
    key_heads = keys.reshape(key_rows, heads, -1)
    value_heads = values.reshape(key_rows, heads, -1)
    score = (
        jnp.einsum("qhe,khe->hqk", query, key_heads, preferred_element_type=jnp.float32) * inverse
        + bias[None, None, :]
    )
    new_top = jnp.maximum(top, jnp.max(score, axis=-1))
    probs = jnp.exp(score - new_top[:, :, None])
    total = jnp.sum(probs, axis=-1)
    update = jnp.einsum(
        "hqk,khe->hqe", probs.astype(jnp.bfloat16), value_heads, preferred_element_type=jnp.float32
    )
    return (new_top, total, update)


def body(tokens, slots, counts, shift, scale, gate, w_qkv, w_out):
    rows, width = tokens.shape
    nblk = rows // BLK
    heads = HEADS
    head_size = width // heads
    inverse = 1.0 / head_size**0.5
    onehot = slots.reshape(nblk, BLK)[:, :, None] == jnp.arange(BLK, dtype=jnp.int32)[None, None, :]
    sums = jnp.einsum(
        "bts,btd->bsd",
        onehot.astype(jnp.bfloat16),
        tokens.reshape(nblk, BLK, width),
        preferred_element_type=jnp.float32,
    )
    members = jnp.sum(onehot.astype(jnp.float32), axis=1)
    merged = (
        (sums / jnp.maximum(members, 1.0)[:, :, None]).astype(jnp.bfloat16).reshape(rows, width)
    )
    normed = layer_norm(merged, shift, scale)
    sizes = members.reshape(rows).astype(jnp.bfloat16)
    qkv = jnp.dot(normed, w_qkv, preferred_element_type=jnp.float32)
    query = qkv[:, :width].astype(jnp.bfloat16)
    keys = qkv[:, width : 2 * width].astype(jnp.bfloat16)
    values = qkv[:, 2 * width :].astype(jnp.bfloat16)
    alive = (
        (jnp.arange(BLK, dtype=jnp.int32)[None, :] < counts[:, None])
        .reshape(rows)
        .astype(jnp.bfloat16)
    )
    query_heads = query.reshape(rows, heads, head_size)
    keys_part = lax.all_gather(keys, "patch", axis=0, tiled=True)
    values_part = lax.all_gather(values, "patch", axis=0, tiled=True)
    sizes_part = lax.all_gather(sizes, "patch", axis=0, tiled=True)
    alive_part = lax.all_gather(alive, "patch", axis=0, tiled=True)
    bias = jnp.where(alive_part > 0, size_bias(sizes_part), -1e30)
    top, total, accum = attend_piece(
        query_heads, empty_carry(heads, rows, head_size), keys_part, values_part, bias, inverse
    )
    attended = finish(accum, total)
    projected = jnp.dot(attended, w_out, preferred_element_type=jnp.float32)
    branch = jnp.einsum(
        "bts,bsd->btd",
        onehot.astype(jnp.float32),
        projected.reshape(nblk, BLK, width),
        precision=lax.Precision.HIGHEST,
    ).reshape(rows, width)
    return (tokens.astype(jnp.float32) + gate * branch).astype(jnp.bfloat16)


def solution(mesh):
    return jax.shard_map(
        body,
        mesh=mesh,
        in_specs=(
            P(("batch", "patch"), None),
            P(("batch", "patch")),
            P(("batch", "patch")),
            P(),
            P(),
            P(),
            P(),
            P(),
        ),
        out_specs=P(("batch", "patch"), None),
        check_vma=False,
    )
```

profile of v0, /device:TPU:0, one launch (start us, length us, event | category | flops | bytes accessed | tf_op | source)
XLA Modules:
  0.0 205.7 jit_solution(10820672473933980348)
XLA Ops:
  6.5 0.0 copy-start
  6.5 0.0 all-gather.5.cloned.1.call-start
  6.5 0.9 convert_reduce_fusion
  7.5 1.4 fusion.27
  8.9 0.2 multiply_reduce_fusion
  9.1 0.7 broadcast_add_fusion
  9.8 4.7 %convolution_convert_fusion = bf16[128,3456]{1,0:T(8,128)(2,1)S(1)} fusion(bf16[1152,3456]{1,0:T(8,128)(2,1)} %param.14, f32[128,1152]{1,0:T(8,128)S(1)} %get-tuple-element.11, f32[1152]{0:T(1024)} %param.11, f32[1152]{0:T(1024)S(1)} %broadcast_add_fusion, f32[128]{0:T(128)S(1)} %add_rsqrt_fusion, f32[128]{0:T(128)S(1)} %broadcast_multiply_fusion), kind=kOutput, calls=%fused_computation.6 | convolution fusion | flops 1020395520 | bytes 9447424 | tf_op jit(solution)/shard_map/dot_general | solution.py:79
  14.5 0.9 fusion.26
  15.4 0.0 all-gather.5.cloned.1.call-update
  15.4 0.0 all-gather.7.cloned.1.call-start
  15.5 0.7 all-gather.7.cloned.1.call-update
  16.2 0.2 copy.18
  17.1 42.7 %all-gather.1 = bf16[16,1,128]{2,1,0:T(2,128)(2,1)S(1)} all-gather(bf16[1,1,128]{2,1,0:T(2,128)(2,1)S(1)} %get-tuple-element.8), channel_id=1, replica_groups=mesh['patch'=16,'batch'=2] {'patch'}, dimensions={0}, use_global_device_ids=true | all-gather | bytes 4352 | tf_op jit(solution)/shard_map/all_gather | solution.py:91
  59.7 36.4 %all-gather = bf16[16,1,128]{2,1,0:T(2,128)(2,1)S(1)} all-gather(bf16[1,1,128]{2,1,0:T(2,128)(2,1)S(1)} %fusion.24), channel_id=1, replica_groups=mesh['patch'=16,'batch'=2] {'patch'}, dimensions={0}, use_global_device_ids=true | all-gather | bytes 4352 | tf_op jit(solution)/shard_map/all_gather | solution.py:92
  96.1 2.0 all-gather.5.cloned.1.call-done
  98.1 6.7 %copy.19 = bf16[2048,1152]{0,1:T(8,128)(2,1)} copy(bf16[2048,1152]{1,0:T(8,128)(2,1)} %all-gather.5.cloned.1.call-done) | data formatting | bytes 9437184 | tf_op jit(solution)/shard_map/all_gather | solution.py:89
  104.9 4.5 %fusion = (f32[16,128]{1,0:T(8,128)S(1)}, f32[16,128,2048]{2,1,0:T(8,128)S(1)}) fusion(f32[2048]{0:T(1024)S(1)} %bitcast.30, bf16[128,16,72]{0,2,1:T(8,128)(2,1)S(1)} %bitcast.28, bf16[2048,16,72]{0,2,1:T(8,128)(2,1)} %bitcast.26), kind=kOutput, calls=%fused_computation.2 | convolution fusion | flops 616560640 | bytes 21807104 | tf_op jit(solution)/shard_map/qhe,khe->hqk/dot_general | solution.py:48
  109.3 0.0 copy-start.1
  109.4 5.7 %copy-done.1 = f32[16,128,2048]{2,1,0:T(8,128)} copy-done((f32[16,128,2048]{2,1,0:T(8,128)}, f32[16,128,2048]{2,1,0:T(8,128)S(1)}, u32[]{:S(2)}) %copy-start.1) | copy-done | bytes 16777240
  115.1 3.8 %fusion.1 = f32[16,128]{1,0:T(8,128)S(1)} fusion(f32[16,128,2048]{2,1,0:T(8,128)S(1)} %get-tuple-element.13, f32[16,128]{1,0:T(8,128)S(1)} %broadcast_maximum_fusion, f32[2048]{0:T(1024)S(1)} %bitcast.31), kind=kLoop, calls=%fused_computation.3 | loop fusion | flops 16775168 | bytes 16801792 | tf_op jit(solution)/shard_map/reduce_sum | solution.py:53
  118.8 60.6 %all-gather.7.cloned.1.call-done = bf16[2048,1152]{1,0:T(8,128)(2,1)} async-done(((bf16[128,1152]{1,0:T(8,128)(2,1)}), bf16[2048,1152]{1,0:T(8,128)(2,1)}) %all-gather.7.cloned.1.call-update) | async-done | bytes 4718608 | tf_op jit(solution)/shard_map/all_gather | solution.py:90
  179.4 6.7 %copy.20 = bf16[2048,1152]{0,1:T(8,128)(2,1)} copy(bf16[2048,1152]{1,0:T(8,128)(2,1)} %all-gather.7.cloned.1.call-done) | data formatting | bytes 9437184 | tf_op jit(solution)/shard_map/all_gather | solution.py:90
  186.1 0.0 copy-start.2
  186.1 0.0 copy-start.3
  186.1 0.0 copy-start.4
  186.1 10.9 %fusion.15 = bf16[128,16,72]{0,2,1:T(8,128)(2,1)S(1)} fusion(bf16[2048,16,72]{0,2,1:T(8,128)(2,1)} %bitcast.27, f32[16,128,2048]{2,1,0:T(8,128)} %copy-done.1, f32[16,128]{1,0:T(8,128)S(1)} %broadcast_maximum_fusion, f32[2048]{0:T(1024)S(1)} %bitcast.32, f32[128,16]{0,1:T(8,128)S(1)} %bitcast.33), kind=kOutput, calls=%fused_computation.15 | convolution fusion | flops 621051904 | bytes 21815296 | tf_op jit(solution)/shard_map/hqk,khe->hqe/dot_general | solution.py:54
  197.0 0.0 copy-done
  197.0 0.6 fusion.28
  197.6 0.0 copy-done.2
  197.6 0.0 copy-done.3
  197.7 0.0 copy-done.4
  197.7 1.2 fusion.8
  (6 shorter events, 0.1 us)
Async XLA Ops:
  6.5 190.5 %copy-start = (bf16[1152,1152]{1,0:T(8,128)(2,1)S(1)}, bf16[1152,1152]{1,0:T(8,128)(2,1)}, u32[]{:S(2)}) copy-start(bf16[1152,1152]{1,0:T(8,128)(2,1)} %param.15) | copy-start | bytes 7962628
  6.5 91.6 %all-gather.5.cloned.1.call-start = ((), (), s32[]{:S(2)}) async-start(), calls=%async_computation | async-start | bytes 5013504 | tf_op jit(solution)/shard_map/all_gather | solution.py:89
  15.4 163.9 %all-gather.7.cloned.1.call-start = ((), (), s32[]{:S(2)}) async-start(), calls=%async_computation.1 | async-start | bytes 5013504 | tf_op jit(solution)/shard_map/all_gather | solution.py:90
  109.3 5.7 %copy-start.1 = (f32[16,128,2048]{2,1,0:T(8,128)}, f32[16,128,2048]{2,1,0:T(8,128)S(1)}, u32[]{:S(2)}) copy-start(f32[16,128,2048]{2,1,0:T(8,128)S(1)} %get-tuple-element.13) | copy-start | bytes 50331652
  186.1 11.5 %copy-start.2 = (bf16[128,1152]{1,0:T(8,128)(2,1)S(1)}, bf16[128,1152]{1,0:T(8,128)(2,1)}, u32[]{:S(2)}) copy-start(bf16[128,1152]{1,0:T(8,128)(2,1)} %param.8) | copy-start | bytes 884740
  186.1 11.5 %copy-start.3 = (f32[1152]{0:T(1024)S(1)}, f32[1152]{0:T(1024)}, u32[]{:S(2)}) copy-start(f32[1152]{0:T(1024)} %param.13) | copy-start | bytes 13828
  186.1 11.5 %copy-start.4 = (s32[128]{0:T(128)S(1)}, s32[128]{0:T(128)}, u32[]{:S(2)}) copy-start(s32[128]{0:T(128)} %param.9) | copy-start | bytes 1540
Sparse Core Ops, SparseCore 0:
  15.6 82.5 all-gather.4
  100.9 78.4 all-gather.6
where the time goes:
time: 206 us
  blocking collectives  79 us (38%)
  waiting for transfers between devices  63.3 us (31%)
  matrix products  23.3 us (11%)
  local copies, waits for them, and re-layouts  20.3 us (10%)
  between operations  14.2 us (7%)
  other arithmetic  5.63 us (3%)
    all_gather x1, waiting for transfers between devices, body(): values_part = lax.all_gather(values, 'patch', axis=0, tiled=True)  60.6 us
    all_gather x1, blocking collectives, body(): sizes_part = lax.all_gather(sizes, 'patch', axis=0, tiled=True)  42.7 us
    all_gather x1, blocking collectives, body(): alive_part = lax.all_gather(alive, 'patch', axis=0, tiled=True)  36.4 us
    dot_general x1, matrix products, attend_piece(): jnp.einsum('hqk,khe->hqe', probs.astype(jnp.bfloat16), value_heads, prefe...  10.9 us
    all_gather x1, local copies, waits for them, and re-layouts, body(): values_part = lax.all_gather(values, 'patch', axis=0, tiled=True)  6.74 us
    all_gather x1, local copies, waits for them, and re-layouts, body(): keys_part = lax.all_gather(keys, 'patch', axis=0, tiled=True)  6.74 us
    unnamed x10, local copies, waits for them, and re-layouts  5.71 us
    dot_general x1, matrix products, body(): qkv = jnp.dot(normed, w_qkv, preferred_element_type=jnp.float32)  4.71 us
  transfers between devices with their start and end apart: 2, of which 2 were waited for; matrix products, arithmetic and copies ran while one was open for 7% of the time, Pallas kernels for 0%

commit v1 on v0

v1 whole, which is shorter than its diff:
```python
import functools
import math

import jax
import jax.numpy as jnp
from jax import lax
from jax.experimental import pallas as pl
from jax.experimental.pallas import tpu as pltpu
from jax.sharding import PartitionSpec as P

HEADS = 16
BLK = 128
AUG = 8
CHUNK = 384
MESH = pl.DeviceIdType.MESH


def layer_norm(merged, shift, scale):
    values = merged.astype(jnp.float32)
    center = jnp.mean(values, axis=-1, keepdims=True)
    spread = jnp.mean((values - center) ** 2, axis=-1, keepdims=True)
    return ((values - center) * lax.rsqrt(spread + 1e-06) * (1.0 + scale) + shift).astype(
        jnp.bfloat16
    )


def merge(tokens, slots, counts):
    rows, width = tokens.shape
    nblk = rows // BLK
    onehot = slots.reshape(nblk, BLK)[:, :, None] == jnp.arange(BLK, dtype=jnp.int32)[None, None, :]
    sums = jnp.einsum(
        "bts,btd->bsd",
        onehot.astype(jnp.bfloat16),
        tokens.reshape(nblk, BLK, width),
        preferred_element_type=jnp.float32,
    )
    members = jnp.sum(onehot.astype(jnp.float32), axis=1)
    merged = (
        (sums / jnp.maximum(members, 1.0)[:, :, None]).astype(jnp.bfloat16).reshape(rows, width)
    )
    alive = (jnp.arange(BLK, dtype=jnp.int32)[None, :] < counts[:, None]).reshape(rows)
    bias = jnp.where(alive, jnp.log(jnp.maximum(members, 1.0)).reshape(rows), -1e30)
    return onehot, merged, bias


def attention(
    n, hd, slots, counts, tokens, shift, scale, w_hbm, out, w, turned, kq_msg, v_msg,
    kq_in, v_in, qs, ks, vs, probs, part, w_sem, *sems
):
    kq_out_sem, kq_in_sem, v_out_sem, v_in_sem, r_out_sem, r_in_sem = sems
    me = lax.axis_index("patch")
    rows, width = tokens.shape
    aug = hd + AUG

    def weights(p):
        return pltpu.make_async_copy(w_hbm.at[:, pl.ds(p * width, width)], w.at[p], w_sem.at[p])

    for p in (1, 0, 2):
        weights(p).start()
    barrier = pltpu.get_barrier_semaphore()
    for i in range(1, n):
        pl.semaphore_signal(
            barrier, inc=1, device_id={"patch": lax.rem(me + i, n)}, device_id_type=MESH
        )

    onehot = slots[...] == lax.broadcasted_iota(jnp.int32, (rows, rows), 0)
    exact = onehot.astype(jnp.float32)
    picks = exact.astype(jnp.bfloat16)
    sums = jnp.dot(picks, tokens[...], preferred_element_type=jnp.float32)
    members = jnp.sum(exact, axis=1, keepdims=True)
    merged = (sums / jnp.maximum(members, 1.0)).astype(jnp.bfloat16)
    normed = layer_norm(merged, shift[...], scale[...])
    sizes = lax.dot_general(
        jnp.ones((AUG, rows), jnp.bfloat16),
        picks,
        (((1,), (1,)), ((), ())),
        preferred_element_type=jnp.float32,
    )
    alive = lax.broadcasted_iota(jnp.int32, (AUG, rows), 1) < counts[...]
    lift = jnp.where(alive, jnp.log(jnp.maximum(sizes, 1.0)), -1e30) * math.sqrt(hd)
    high = lift.astype(jnp.bfloat16).astype(jnp.float32)
    rest = lift - high
    middle = rest.astype(jnp.bfloat16).astype(jnp.float32)
    low = rest - middle
    line = lax.broadcasted_iota(jnp.int32, (AUG, rows), 0)
    extra = jnp.where(
        line == 0, high, jnp.where(line == 1, middle, jnp.where(line == 2, low, 0.0))
    )

    def project(p):
        weights(p).wait()
        for at in range(0, width, CHUNK):
            piece = jnp.dot(normed, w[p, :, at : at + CHUNK], preferred_element_type=jnp.float32)
            turned[at : at + CHUNK] = piece.T

    def head(h):
        return turned[h * hd : (h + 1) * hd]

    project(1)
    for h in range(n):
        kq_msg[h, :aug] = jnp.concatenate([head(h), extra], axis=0).astype(jnp.bfloat16)
    project(0)
    for h in range(n):
        kq_msg[h, aug:] = head(h).astype(jnp.bfloat16)

    def copy(src_ref, dst_ref, send, recv, dst, src):
        return pltpu.make_async_remote_copy(
            src_ref=src_ref.at[dst],
            dst_ref=dst_ref.at[src],
            send_sem=send.at[dst],
            recv_sem=recv.at[src],
            device_id={"patch": dst},
            device_id_type=MESH,
        )

    def kq_to(dst, src):
        return copy(kq_msg, kq_in, kq_out_sem, kq_in_sem, dst, src)

    def v_to(dst, src):
        return copy(v_msg, v_in, v_out_sem, v_in_sem, dst, src)

    def result_to(dst, src):
        return copy(part, out, r_out_sem, r_in_sem, dst, src)

    pl.semaphore_wait(barrier, n - 1)
    for i in range(1, n):
        kq_to(lax.rem(me + i, n), me).start()
    project(2)
    for h in range(n):
        v_msg[h] = head(h).astype(jnp.bfloat16)
    for i in range(1, n):
        v_to(lax.rem(me + i, n), me).start()

    tail = jnp.ones((AUG, rows), jnp.bfloat16)

    def columns(src):
        return pl.ds(pl.multiple_of(src * rows, rows), rows)

    def place_kq(src, block):
        ks[:, columns(src)] = block[:aug]
        qs[:, columns(src)] = jnp.concatenate([block[aug:], tail], axis=0)

    def place_v(src, block):
        vs[:, columns(src)] = jnp.concatenate([block, tail], axis=0)

    place_kq(me, kq_msg[me])
    for i in range(1, n):
        src = lax.rem(me + n - i, n)
        kq_to(src, src).wait_recv()
        place_kq(src, kq_in[src])

    factor = math.log2(math.e) / math.sqrt(hd)
    wide = 2 * rows
    pairs = n // 2

    def pair_of(c):
        return lax.rem(me // 2 + c, pairs)

    def send_pair(c):
        for t in range(2):
            dst = 2 * pair_of(c) + t

            @pl.when(dst != me)
            def _():
                result_to(dst, me).start()

            @pl.when(dst == me)
            def _():
                out[me] = part[me]

    def weigh(c, _):
        query = qs[:, pl.ds(pl.multiple_of(pair_of(c) * wide, wide), wide)]
        score = lax.dot_general(
            ks[...], query, (((0,), (0,)), ((), ())), preferred_element_type=jnp.float32
        )
        top = jnp.max(score, axis=0, keepdims=True)
        probs[c] = jnp.exp2((score - top) * factor).astype(jnp.bfloat16)
        return 0

    lax.fori_loop(0, pairs, weigh, 0)

    place_v(me, v_msg[me])
    for i in range(1, n):
        src = lax.rem(me + n - i, n)
        v_to(src, src).wait_recv()
        place_v(src, v_in[src])

    def finish(c, _):
        first = pair_of(c)
        acc = jnp.dot(vs[...], probs[c], preferred_element_type=jnp.float32)
        done = (acc[:hd] / acc[hd : hd + 1]).astype(jnp.bfloat16)
        part[2 * first] = done[:, :rows]
        part[2 * first + 1] = done[:, rows:]

        @pl.when(c > 0)
        def _():
            send_pair(c - 1)

        return 0

    lax.fori_loop(0, pairs, finish, 0)
    send_pair(pairs - 1)

    for i in range(1, n):
        other = lax.rem(me + i, n)
        kq_to(other, me).wait_send()
        v_to(other, me).wait_send()
        result_to(other, me).wait_send()
        src = lax.rem(me + n - i, n)
        result_to(src, src).wait_recv()


def heads_apart(n, width, tokens, slots, counts, shift, scale, gate, w_qkv, w_out):
    rows = tokens.shape[0]
    hd = width // HEADS
    aug = hd + AUG
    vmem = pl.BlockSpec(memory_space=pltpu.VMEM)
    attended = pl.pallas_call(
        functools.partial(attention, n, hd),
        out_shape=jax.ShapeDtypeStruct((n, hd, rows), jnp.bfloat16),
        in_specs=[vmem] * 5 + [pl.BlockSpec(memory_space=pl.ANY)],
        out_specs=vmem,
        scratch_shapes=[
            pltpu.VMEM((3, width, width), jnp.bfloat16),
            pltpu.VMEM((width, rows), jnp.float32),
            pltpu.VMEM((n, aug + hd, rows), jnp.bfloat16),
            pltpu.VMEM((n, hd, rows), jnp.bfloat16),
            pltpu.VMEM((n, aug + hd, rows), jnp.bfloat16),
            pltpu.VMEM((n, hd, rows), jnp.bfloat16),
            pltpu.VMEM((aug, n * rows), jnp.bfloat16),
            pltpu.VMEM((aug, n * rows), jnp.bfloat16),
            pltpu.VMEM((aug, n * rows), jnp.bfloat16),
            pltpu.VMEM((n // 2, n * rows, 2 * rows), jnp.bfloat16),
            pltpu.VMEM((n, hd, rows), jnp.bfloat16),
            pltpu.SemaphoreType.DMA((3,)),
        ]
        + [pltpu.SemaphoreType.DMA((n,))] * 6,
        compiler_params=pltpu.CompilerParams(
            collective_id=0, has_side_effects=True, vmem_limit_bytes=56 * 1024 * 1024
        ),
    )(slots[None], counts[None], tokens, shift[None], scale[None], w_qkv)
    attended = attended.reshape(width, rows)
    onehot = slots[:, None] == jnp.arange(rows, dtype=jnp.int32)[None, :]
    picked = lax.dot_general(
        onehot.astype(jnp.bfloat16),
        attended,
        (((1,), (1,)), ((), ())),
        preferred_element_type=jnp.float32,
    ).astype(jnp.bfloat16)
    branch = jnp.dot(picked, w_out, preferred_element_type=jnp.float32)
    return (tokens.astype(jnp.float32) + gate * branch).astype(jnp.bfloat16)


def rows_gathered(tokens, slots, counts, shift, scale, gate, w_qkv, w_out):
    rows, width = tokens.shape
    nblk = rows // BLK
    hd = width // HEADS
    onehot, merged, bias = merge(tokens, slots, counts)
    normed = layer_norm(merged, shift, scale)
    qkv = jnp.dot(normed, w_qkv, preferred_element_type=jnp.float32)
    query, keys, values = (
        qkv[:, i * width : (i + 1) * width].astype(jnp.bfloat16) for i in range(3)
    )
    keys = lax.all_gather(keys, "patch", axis=0, tiled=True).reshape(-1, HEADS, hd)
    values = lax.all_gather(values, "patch", axis=0, tiled=True).reshape(-1, HEADS, hd)
    bias = lax.all_gather(bias, "patch", axis=0, tiled=True)
    query = query.reshape(rows, HEADS, hd)
    score = jnp.einsum("qhe,khe->hqk", query, keys, preferred_element_type=jnp.float32)
    score = score / hd**0.5 + bias[None, None, :]
    probs = jnp.exp(score - jnp.max(score, axis=-1, keepdims=True))
    total = jnp.sum(probs, axis=-1)
    update = jnp.einsum(
        "hqk,khe->hqe", probs.astype(jnp.bfloat16), values, preferred_element_type=jnp.float32
    )
    attended = (update / total[:, :, None]).transpose(1, 0, 2).reshape(rows, width)
    picked = jnp.einsum(
        "bts,bsd->btd",
        onehot.astype(jnp.bfloat16),
        attended.astype(jnp.bfloat16).reshape(nblk, BLK, width),
        preferred_element_type=jnp.float32,
    ).astype(jnp.bfloat16)
    branch = jnp.dot(picked.reshape(rows, width), w_out, preferred_element_type=jnp.float32)
    return (tokens.astype(jnp.float32) + gate * branch).astype(jnp.bfloat16)


def solution(mesh):
    n = mesh.shape["patch"]

    def body(tokens, *rest):
        if n == HEADS and tokens.shape[0] == BLK:
            return heads_apart(n, tokens.shape[1], tokens, *rest)
        return rows_gathered(tokens, *rest)

    return jax.shard_map(
        body,
        mesh=mesh,
        in_specs=(
            P(("batch", "patch"), None),
            P(("batch", "patch")),
            P(("batch", "patch")),
            P(),
            P(),
            P(),
            P(),
            P(),
        ),
        out_specs=P(("batch", "patch"), None),
        check_vma=False,
    )
```

time: 206 us -> 48.2 us (0.23)
  blocking collectives: 79 us -> 0 us
  waiting for transfers between devices: 63.3 us -> 0 us
  Pallas kernels: 0 us -> 42.1 us
  matrix products: 23.3 us -> 2.45 us
  local copies, waits for them, and re-layouts: 20.3 us -> 2.6 us
  between operations: 14.2 us -> 0.85 us
  other arithmetic: 5.63 us -> 0 us
    all_gather x2 -> x0, blocking collectives: 79 us -> none  [the longest x1 42.7 us: body(): sizes_part = lax.all_gather(sizes, 'patch', axis=0, tiled=True)]
    all_gather x2 -> x0, waiting for transfers between devices: 62.6 us -> none  [the longest x1 60.6 us: body(): values_part = lax.all_gather(values, 'patch', axis=0, tiled=True)]
    pallas_call x0 -> x1, Pallas kernels: none -> 42.1 us  [heads_apart(): pl.pallas_call(functools.partial(attention, n, hd), out_shape=jax.ShapeDt...]
    dot_general x6 -> x1, matrix products: 23.3 us -> 2.45 us  [heads_apart(): branch = jnp.dot(picked, w_out, preferred_element_type=jnp.float32)]
    all_gather x2 -> x0, local copies, waits for them, and re-layouts: 13.5 us -> none  [the longest x1 6.74 us: body(): values_part = lax.all_gather(values, 'patch', axis=0, tiled=True)]
    unnamed x10 -> x8, local copies, waits for them, and re-layouts: 5.71 us -> 0.02 us
    reduce_sum x3 -> x0, other arithmetic: 4.87 us -> none  [the longest x1 3.76 us: attend_piece(): total = jnp.sum(probs, axis=-1)]
    broadcast_in_dim x0 -> x2, local copies, waits for them, and re-layouts: none -> 2.59 us  [the longest x1 1.3 us: heads_apart(): shift[None]]
  transfers between devices with their start and end apart: 2 -> 0, of which waited for: 2 -> 0; matrix products, arithmetic and copies ran while one was open for 7% -> 0% of each run, Pallas kernels for 0% -> 0%
where the time goes in v1:
time: 48.2 us; the launch traced here: 48 us
  Pallas kernels  42.1 us (87%)
  local copies, waits for them, and re-layouts  2.6 us (5%)
  matrix products  2.45 us (5%)
  between operations  0.85 us (2%)
    pallas_call x1, Pallas kernels, heads_apart(): pl.pallas_call(functools.partial(attention, n, hd), out_shape=jax.ShapeDt...  42.1 us
    dot_general x1, matrix products, heads_apart(): branch = jnp.dot(picked, w_out, preferred_element_type=jnp.float32)  2.45 us
    broadcast_in_dim x1, local copies, waits for them, and re-layouts, heads_apart(): shift[None]  1.3 us
    broadcast_in_dim x1, local copies, waits for them, and re-layouts, heads_apart(): scale[None]  1.29 us

profile of v1, /device:TPU:0, one launch (start us, length us, event | category | flops | bytes accessed | tf_op | source)
XLA Modules:
  0.0 48.0 jit_solution(785507438264791596)
XLA Ops:
  0.0 0.0 copy-start
  0.8 1.3 %broadcast_in_dim.17.shift = f32[1,1152]{1,0:T(1,128)} reshape(f32[1152]{0:T(1024)} %param.11) | data formatting | bytes 9216 | tf_op jit(solution)/shard_map/broadcast_in_dim | solution.py:241
  2.1 1.3 %broadcast_in_dim.18.scale = f32[1,1152]{1,0:T(1,128)} reshape(f32[1152]{0:T(1024)} %param.12) | data formatting | bytes 9216 | tf_op jit(solution)/shard_map/broadcast_in_dim | solution.py:241
  3.4 0.0 copy-start.1
  3.4 0.0 copy-start.2
  3.4 0.0 copy-start.3
  3.4 42.1 %shard_map.82 = bf16[16,72,128]{2,1,0:T(8,128)(2,1)} custom-call(s32[1,128]{1,0:T(1,128)} %bitcast.7, s32[1,1]{1,0:T(1,128)} %bitcast.5.counts, bf16[128,1152]{1,0:T(8,128)(2,1)} %tokens.1, f32[1,1152]{1,0:T(1,128)} %broadcast_in_dim.17.shift, f32[1,1152]{1,0:T(1,128)} %broadcast_in_dim.18.scale, bf16[1152,3456]{1,0:T(8,128)(2,1)} %w_hbm.1), custom_call_target="tpu_custom_call" | custom-call | tf_op jit(solution)/shard_map/pallas_call | solution.py:218
  45.5 0.0 copy-done
  45.5 0.0 copy-done.1
  45.5 0.0 copy-done.2
  45.5 0.0 copy-done.3
  45.5 2.5 %fusion.1 = bf16[128,1152]{1,0:T(8,128)(2,1)} fusion(bf16[1152,1152]{1,0:T(8,128)(2,1)S(1)} %copy-done, bf16[1152,128]{1,0:T(8,128)(2,1)} %bitcast.6, bf16[128,1152]{1,0:T(8,128)(2,1)S(1)} %copy-done.1, f32[1152]{0:T(1024)S(1)} %copy-done.2, s32[128]{0:T(128)S(1)} %copy-done.3), kind=kOutput, calls=%fused_computation.2 | convolution fusion | flops 378241024 | bytes 3544064 | tf_op jit(solution)/shard_map/dot_general | solution.py:250
Async XLA Ops:
  0.0 45.5 %copy-start = (bf16[1152,1152]{1,0:T(8,128)(2,1)S(1)}, bf16[1152,1152]{1,0:T(8,128)(2,1)}, u32[]{:S(2)}) copy-start(bf16[1152,1152]{1,0:T(8,128)(2,1)} %param.15) | copy-start | bytes 7962628
  3.4 42.1 %copy-start.1 = (bf16[128,1152]{1,0:T(8,128)(2,1)S(1)}, bf16[128,1152]{1,0:T(8,128)(2,1)}, u32[]{:S(2)}) copy-start(bf16[128,1152]{1,0:T(8,128)(2,1)} %tokens.1) | copy-start | bytes 884740
  3.4 42.1 %copy-start.2 = (f32[1152]{0:T(1024)S(1)}, f32[1152]{0:T(1024)}, u32[]{:S(2)}) copy-start(f32[1152]{0:T(1024)} %param.13) | copy-start | bytes 13828
  3.4 42.1 %copy-start.3 = (s32[128]{0:T(128)S(1)}, s32[128]{0:T(128)}, u32[]{:S(2)}) copy-start(s32[128]{0:T(128)} %param.9) | copy-start | bytes 1540

commit v2 on v1

--- a/solution.py
+++ b/solution.py
@@ -69,7 +69,7 @@
     sums = jnp.dot(picks, tokens[...], preferred_element_type=jnp.float32)
     members = jnp.sum(exact, axis=1, keepdims=True)
     merged = (sums / jnp.maximum(members, 1.0)).astype(jnp.bfloat16)
-    normed = layer_norm(merged, shift[...], scale[...])
+    normed = layer_norm(merged, shift[...][None], scale[...][None])
     sizes = lax.dot_general(
         jnp.ones((AUG, rows), jnp.bfloat16),
         picks,
@@ -238,7 +238,7 @@
         compiler_params=pltpu.CompilerParams(
             collective_id=0, has_side_effects=True, vmem_limit_bytes=56 * 1024 * 1024
         ),
-    )(slots[None], counts[None], tokens, shift[None], scale[None], w_qkv)
+    )(slots[None], counts[None], tokens, shift, scale, w_qkv)
     attended = attended.reshape(width, rows)
     onehot = slots[:, None] == jnp.arange(rows, dtype=jnp.int32)[None, :]
     picked = lax.dot_general(

time: 48.2 us -> 45.5 us (0.944)
  local copies, waits for them, and re-layouts: 2.6 us -> 0.02 us
    broadcast_in_dim x2 -> x0, local copies, waits for them, and re-layouts: 2.59 us -> none  [the longest x1 1.3 us: heads_apart(): shift[None]]
where the time goes in v2:
time: 45.5 us; the launch traced here: 45.4 us
  Pallas kernels  42.1 us (93%)
  matrix products  2.45 us (5%)
  between operations  0.87 us (2%)
    pallas_call x1, Pallas kernels, heads_apart(): pl.pallas_call(functools.partial(attention, n, hd), out_shape=jax.ShapeDt...  42.1 us
    dot_general x1, matrix products, heads_apart(): branch = jnp.dot(picked, w_out, preferred_element_type=jnp.float32)  2.45 us

profile of v2, /device:TPU:0, one launch (start us, length us, event | category | flops | bytes accessed | tf_op | source)
XLA Modules:
  0.0 45.4 jit_solution(10814832462270586521)
XLA Ops:
  0.0 0.0 copy-start
  0.8 0.0 copy-start.1
  0.8 0.0 copy-start.2
  0.8 0.0 copy-start.3
  0.8 42.1 %shard_map.82 = bf16[16,72,128]{2,1,0:T(8,128)(2,1)} custom-call(s32[1,128]{1,0:T(1,128)} %bitcast.7, s32[1,1]{1,0:T(1,128)} %bitcast.5.counts, bf16[128,1152]{1,0:T(8,128)(2,1)} %tokens.1, f32[1152]{0:T(1024)} %shift.1, f32[1152]{0:T(1024)} %scale.1, bf16[1152,3456]{1,0:T(8,128)(2,1)} %w_hbm.1), custom_call_target="tpu_custom_call" | custom-call | tf_op jit(solution)/shard_map/pallas_call | solution.py:218
  42.9 0.0 copy-done
  42.9 0.0 copy-done.1
  42.9 0.0 copy-done.2
  42.9 0.0 copy-done.3
  42.9 2.5 %fusion.1 = bf16[128,1152]{1,0:T(8,128)(2,1)} fusion(bf16[1152,1152]{1,0:T(8,128)(2,1)S(1)} %copy-done, bf16[1152,128]{1,0:T(8,128)(2,1)} %bitcast.6, bf16[128,1152]{1,0:T(8,128)(2,1)S(1)} %copy-done.1, f32[1152]{0:T(1024)S(1)} %copy-done.2, s32[128]{0:T(128)S(1)} %copy-done.3), kind=kOutput, calls=%fused_computation.2 | convolution fusion | flops 378241024 | bytes 3544064 | tf_op jit(solution)/shard_map/dot_general | solution.py:250
Async XLA Ops:
  0.0 42.9 %copy-start = (bf16[1152,1152]{1,0:T(8,128)(2,1)S(1)}, bf16[1152,1152]{1,0:T(8,128)(2,1)}, u32[]{:S(2)}) copy-start(bf16[1152,1152]{1,0:T(8,128)(2,1)} %param.15) | copy-start | bytes 7962628
  0.8 42.1 %copy-start.1 = (bf16[128,1152]{1,0:T(8,128)(2,1)S(1)}, bf16[128,1152]{1,0:T(8,128)(2,1)}, u32[]{:S(2)}) copy-start(bf16[128,1152]{1,0:T(8,128)(2,1)} %tokens.1) | copy-start | bytes 884740
  0.8 42.1 %copy-start.2 = (f32[1152]{0:T(1024)S(1)}, f32[1152]{0:T(1024)}, u32[]{:S(2)}) copy-start(f32[1152]{0:T(1024)} %param.13) | copy-start | bytes 13828
  0.8 42.1 %copy-start.3 = (s32[128]{0:T(128)S(1)}, s32[128]{0:T(128)}, u32[]{:S(2)}) copy-start(s32[128]{0:T(128)} %param.9) | copy-start | bytes 1540
